TPU v7x, 32 devices: a whole 2x2x4 slice. The times are simulated.
32 devices in a mesh: dp: 4 (over z), section: 4 (over x, core), head: 2 (over y).
Axes of the slice: x: 2, y: 2, z: 4, core: 2. Of those that a mesh axis runs over, the one named last changes fastest.
Arguments:
- q_latent: bfloat16 [4, 2048, 1536], P('section', 'dp'), may hold values from -6 to 6
- kv_latent: bfloat16 [4, 2048, 576], P('section', 'dp'), may hold values from -6 to 6
- segment_ids: int32 [2048], P('dp'), may hold values from 0 to 31, never falling along the last dimension, each value on 1 to 512 neighbouring positions
- q_weight: bfloat16 [4, 1536, 12288], P('section', 'dp', 'head'), may hold values from -100 to 100
- k_weight: bfloat16 [4, 512, 8192], P('section', None, 'head'), may hold values from -0.25 to 0.25
Outputs:
- logit_ratio: float32 [4, 64], P(None, 'head')
- scaled_q: bfloat16 [4, 1536, 12288], P('section', 'dp', 'head')
- scaled_k: bfloat16 [4, 512, 8192], P('section', None, 'head')
All inputs are finite; a program needn't handle non-finite values.
Results may differ from a plain program's by a relative error of at most 0.0034.
Values may be sent and summed in bfloat16 or wider, within the bound.
A program may use at most 128 MiB of HBM per device.

v0:
```python
import jax
import jax.numpy as jnp
from jax import lax
from jax.sharding import PartitionSpec as P

D_KV = 512
NOPE = 128
ROPE = 64


clip_threshold = 100.0
rope_base = 50000.0


def rotate(values, positions):
    half_width = values.shape[-1] // 2
    frequency = rope_base ** (-jnp.arange(half_width, dtype=jnp.float32) / half_width)
    angles = positions[:, None].astype(jnp.float32) * frequency[None, :]
    cosine = jnp.cos(angles)[:, None, :]
    sine_part = jnp.sin(angles)[:, None, :]
    lower_half = values[..., :half_width]
    upper_half = values[..., half_width:]
    return jnp.concatenate(
        [
            lower_half * cosine - upper_half * sine_part,
            upper_half * cosine + lower_half * sine_part,
        ],
        -1,
    )


def sequence_maxima(q_full, kv_rows, segments, w_key):
    length = kv_rows.shape[0]
    heads_here = w_key.shape[1] // NOPE
    q_full = q_full.reshape(length, heads_here, NOPE + ROPE)
    positions = jnp.arange(length, dtype=jnp.int32)
    queries = jnp.concatenate(
        [q_full[..., :NOPE], rotate(q_full[..., NOPE:], positions)], -1
    ).astype(jnp.bfloat16)
    key_nope = jnp.dot(kv_rows[:, :D_KV], w_key, preferred_element_type=jnp.float32).astype(
        jnp.bfloat16
    )
    key_nope = key_nope.reshape(length, heads_here, NOPE)
    key_rope = jnp.broadcast_to(kv_rows[:, None, D_KV:], (length, heads_here, ROPE))
    keys_all = jnp.concatenate([key_nope, key_rope], -1)
    logits = jnp.einsum("shd,thd->hst", queries, keys_all, preferred_element_type=jnp.float32)
    logits = logits * (NOPE + ROPE) ** (-0.5)
    allowed = (segments[:, None] == segments[None, :]) & (positions[None, :] <= positions[:, None])
    return jnp.max(jnp.where(allowed[None], logits, -1e30), axis=(1, 2))


def scale_weights(own_max, q_weight, k_weight):
    factor = clip_threshold / jnp.maximum(own_max, clip_threshold)
    square_root = jnp.sqrt(factor)
    layers_here, heads_here = own_max.shape
    column_scale = jnp.concatenate(
        [
            jnp.broadcast_to(square_root[..., None], (layers_here, heads_here, NOPE)),
            jnp.broadcast_to(factor[..., None], (layers_here, heads_here, ROPE)),
        ],
        -1,
    )
    rows_q = q_weight.shape[1]
    scaled_q = (
        (
            q_weight.astype(jnp.float32).reshape(layers_here, rows_q, heads_here, NOPE + ROPE)
            * column_scale[:, None]
        )
        .reshape(q_weight.shape)
        .astype(jnp.bfloat16)
    )
    scaled_k = (
        (
            k_weight.astype(jnp.float32).reshape(layers_here, D_KV, heads_here, NOPE)
            * square_root[:, None, :, None]
        )
        .reshape(k_weight.shape)
        .astype(jnp.bfloat16)
    )
    return (scaled_q, scaled_k)


def per_device(q_latent, kv_latent, segment_ids, q_weight, k_weight):
    latent_q = q_latent[0]
    q_full = jnp.dot(
        latent_q,
        lax.all_gather(q_weight[0], "dp", axis=0, tiled=True),
        preferred_element_type=jnp.float32,
    )
    own_rows = [sequence_maxima(q_full, kv_latent[0], segment_ids, k_weight[0])]
    own_max = jnp.stack(own_rows)
    layer_max = lax.pmax(own_max, "dp")
    max_table = lax.all_gather(layer_max, "section", axis=0, tiled=True)
    scaled_q, scaled_k = scale_weights(layer_max, q_weight, k_weight)
    return (max_table / clip_threshold, scaled_q, scaled_k)


def solution(mesh):
    return jax.shard_map(
        per_device,
        mesh=mesh,
        in_specs=(
            P("section", "dp", None),
            P("section", "dp", None),
            P("dp"),
            P("section", "dp", "head"),
            P("section", None, "head"),
        ),
        out_specs=(P(None, "head"), P("section", "dp", "head"), P("section", None, "head")),
        check_vma=False,
    )
```

profile of v0, /device:TPU:0, one launch (start us, length us, event | category | flops | bytes accessed | tf_op | source)
XLA Modules:
  0.0 418.0 jit_solution(13002080678329294674)
XLA Ops:
  7.2 0.0 copy-start
  7.2 0.0 all-gather.4.cloned.1.call-start
  7.2 0.7 all-gather.4.cloned.1.call-update
  7.9 0.8 slice.28
  8.8 6.7 %convolution_convert_fusion = bf16[512,4096]{1,0:T(8,128)(2,1)} fusion(bf16[1,512,4096]{2,1,0:T(8,128)(2,1)} %param.9, bf16[512,576]{0,1:T(8,128)(2,1)} %bitcast.28), kind=kOutput, calls=%fused_computation.12 | convolution fusion | flops 2149580800 | bytes 8912896 | tf_op jit(solution)/shard_map/dot_general | solution.py:40
  15.5 0.0 copy-start.2
  15.5 6.5 %copy.12 = bf16[512,4096]{0,1:T(8,128)(2,1)} copy(bf16[512,4096]{1,0:T(8,128)(2,1)} %convolution_convert_fusion) | data formatting | bytes 8388608 | tf_op jit(solution)/shard_map/reshape | solution.py:43
  22.1 0.3 multiply_cosine_fusion
  22.4 0.0 copy-done.2
  22.4 0.2 fusion.11
  22.6 312.3 %all-gather.4.cloned.1.call-done = bf16[1,1536,6144]{2,1,0:T(8,128)(2,1)} async-done(((bf16[1,384,6144]{2,1,0:T(8,128)(2,1)}), bf16[1,1536,6144]{2,1,0:T(8,128)(2,1)}) %all-gather.4.cloned.1.call-update) | async-done | bytes 18874384 | tf_op jit(solution)/shard_map/all_gather | solution.py:87
  334.9 24.6 %copy.10 = bf16[6144,1536]{1,0:T(8,128)(2,1)} copy(bf16[6144,1536]{0,1:T(8,128)(2,1)} %bitcast.22) | data formatting | bytes 37748736 | tf_op jit(solution)/shard_map/dot_general | solution.py:85
  359.6 0.0 copy-done
  359.6 14.1 %fusion.9 = f32[512,32,192]{0,2,1:T(8,128)S(1)} fusion(bf16[32,192,1536]{2,1,0:T(8,128)(2,1)} %bitcast.23, bf16[1,512,1536]{2,1,0:T(8,128)(2,1)S(1)} %copy-done), kind=kOutput, calls=%fused_computation.16 | convolution fusion | flops 9663676416 | bytes 33030144 | tf_op jit(solution)/shard_map/dot_general | solution.py:85
  373.7 2.6 slice.36
  376.3 0.7 subtract_convert_fusion
  377.0 1.6 broadcast_in_dim.23
  378.6 8.3 %select_reduce_fusion = f32[32]{0:T(128)S(1)} fusion(pred[512,512]{1,0:T(8,128)(4,1)S(1)} %fusion.11, bf16[512,32,32]{0,2,1:T(8,128)(2,1)S(1)} %get-tuple-element.6, bf16[512,32,32]{0,2,1:T(8,128)(2,1)S(1)} %get-tuple-element.5, bf16[512,32,128]{0,2,1:T(8,128)(2,1)} %slice.36, bf16[512,32,64]{0,2,1:T(8,128)(2,1)} %broadcast_in_dim.23, ...), kind=kOutput, calls=%fused_computation | convolution fusion | flops 3277848576 | bytes 12845184 | tf_op jit(solution)/shard_map/shd,thd->hst/dot_general | solution.py:46
  387.0 0.0 slice-start
  387.0 9.4 %pmax.7 = f32[1,32]{1,0:T(1,128)S(1)} all-reduce(f32[1,32]{1,0:T(1,128)S(1)} %bitcast.32), channel_id=1, replica_groups=mesh['dp'=4,'section'=4,'head'=2] {'dp'}, use_global_device_ids=true, to_apply=%region_1.2 | all-reduce | flops 32 | bytes 256 | tf_op jit(solution)/shard_map/pmax | solution.py:92
  396.4 5.1 %all-gather.1 = f32[4,1,32]{2,1,0:T(1,128)S(1)} all-gather(f32[1,1,32]{2,1,0:T(1,128)S(1)} %bitcast.31), channel_id=1, replica_groups=mesh['dp'=4,'section'=4,'head'=2] {'section'}, dimensions={0}, use_global_device_ids=true | all-gather | bytes 640 | tf_op jit(solution)/shard_map/all_gather | solution.py:93
  401.4 0.6 broadcast_multiply_fusion
  402.0 0.1 broadcast_bitcast_fusion
  402.1 0.1 broadcast_in_dim.28
  402.2 0.1 broadcast_in_dim.26
  402.2 0.1 mul.117
  402.3 0.0 slice-start.1
  402.3 0.0 copy-start.1
  402.4 5.4 %multiply_convert_fusion.1 = bf16[1,512,4096]{2,1,0:T(8,128)(2,1)} fusion(bf16[1,512,4096]{2,1,0:T(8,128)(2,1)} %param.9, f32[4096]{0:T(1024)S(1)} %broadcast_bitcast_fusion), kind=kLoop, calls=%fused_computation.3 | loop fusion | flops 6291456 | bytes 8404992 | tf_op jit(solution)/shard_map/convert_element_type | solution.py:78
  407.8 0.0 slice-done
  407.8 0.0 slice-done.1
  407.8 3.4 multiply_convert_fusion
  411.2 0.0 copy-done.1
  (5 shorter events, 0.0 us)
Async XLA Ops:
  7.2 352.4 %copy-start = (bf16[1,512,1536]{2,1,0:T(8,128)(2,1)S(1)}, bf16[1,512,1536]{2,1,0:T(8,128)(2,1)}, u32[]{:S(2)}) copy-start(bf16[1,512,1536]{2,1,0:T(8,128)(2,1)} %param.5) | copy-start | bytes 4718596
  7.2 327.7 %all-gather.4.cloned.1.call-start = ((), (), s32[]{:S(2)}) async-start(), calls=%async_computation | async-start | bytes 23592960 | tf_op jit(solution)/shard_map/all_gather | solution.py:87
  15.5 6.9 %copy-start.2 = (s32[512]{0:T(512)S(1)}, s32[512]{0:T(512)}, u32[]{:S(2)}) copy-start(s32[512]{0:T(512)} %param.7) | copy-start | bytes 6148
  387.0 20.8 %slice-start = ((s8[4718592]{0:T(1024)(128)(4,1)}), s8[524288]{0:T(1024)(128)(4,1)S(1)}, s32[]{:S(2)}) async-start(s8[4718592]{0:T(1024)(128)(4,1)} %bitcast.24), calls=%async_computation.1 | async-start | bytes 1048576
  402.3 5.5 %slice-start.1 = ((s8[4718592]{0:T(1024)(128)(4,1)}), s8[4194304]{0:T(1024)(128)(4,1)S(1)}, s32[]{:S(2)}) async-start(s8[4718592]{0:T(1024)(128)(4,1)} %bitcast.24), calls=%async_computation.2 | async-start | bytes 8388608
  402.3 8.8 %copy-start.1 = (bf16[1,512,1536]{2,1,0:T(8,128)(2,1)S(1)}, bf16[1,512,1536]{2,1,0:T(8,128)(2,1)}, u32[]{:S(2)}) copy-start(bf16[1,512,1536]{2,1,0:T(8,128)(2,1)} %param.5) | copy-start | bytes 4718596
Sparse Core Ops, SparseCore 0:
  9.6 325.2 all-gather.3
where the time goes:
time: 419 us; the launch traced here: 418 us
  waiting for transfers between devices  313 us (75%)
  local copies, waits for them, and re-layouts  36.6 us (9%)
  matrix products  29.2 us (7%)
  blocking collectives  14.5 us (3%)
  between operations  14.1 us (3%)
  other arithmetic  10.7 us (3%)
    all_gather x1, waiting for transfers between devices, per_device(): lax.all_gather(q_weight[0], 'dp', axis=0, tiled=True)  312 us
    dot_general x1, local copies, waits for them, and re-layouts, per_device(): jnp.dot(latent_q, lax.all_gather(q_weight[0], 'dp', axis=0, tiled=True),...  24.6 us
    dot_general x1, matrix products, per_device(): jnp.dot(latent_q, lax.all_gather(q_weight[0], 'dp', axis=0, tiled=True),...  14.1 us
    pmax x1, blocking collectives, per_device(): layer_max = lax.pmax(own_max, 'dp')  9.41 us
  transfers between devices with their start and end apart: 1, of which 1 were waited for; matrix products, arithmetic and copies ran while one was open for 4% of the time, Pallas kernels for 0%

commit v1 on v0

v1 whole, which is shorter than its diff:
```python
import functools
import jax
import jax.numpy as jnp
import numpy as np
from jax import lax
from jax.experimental import pallas as pl
from jax.experimental.pallas import tpu as pltpu
from jax.sharding import PartitionSpec as P

D_KV = 512
NOPE = 128
ROPE = 64
HEAD = NOPE + ROPE
LANES = 128
NEG = -1e30
MESH = pl.DeviceIdType.MESH

clip_threshold = 100.0
rope_base = 50000.0


def rotate(values, positions):
    half_width = values.shape[-1] // 2
    frequency = rope_base ** (-jnp.arange(half_width, dtype=jnp.float32) / half_width)
    angles = positions[:, None].astype(jnp.float32) * frequency[None, :]
    cosine = jnp.cos(angles)[:, None, :]
    sine_part = jnp.sin(angles)[:, None, :]
    lower_half = values[..., :half_width]
    upper_half = values[..., half_width:]
    return jnp.concatenate(
        [
            lower_half * cosine - upper_half * sine_part,
            upper_half * cosine + lower_half * sine_part,
        ],
        -1,
    )


def sequence_maxima(q_full, kv_rows, segments, w_key):
    length = kv_rows.shape[0]
    heads_here = w_key.shape[1] // NOPE
    q_full = q_full.reshape(length, heads_here, HEAD)
    positions = jnp.arange(length, dtype=jnp.int32)
    queries = jnp.concatenate(
        [q_full[..., :NOPE], rotate(q_full[..., NOPE:], positions)], -1
    ).astype(jnp.bfloat16)
    key_nope = jnp.dot(kv_rows[:, :D_KV], w_key, preferred_element_type=jnp.float32).astype(
        jnp.bfloat16
    )
    key_nope = key_nope.reshape(length, heads_here, NOPE)
    key_rope = jnp.broadcast_to(kv_rows[:, None, D_KV:], (length, heads_here, ROPE))
    keys_all = jnp.concatenate([key_nope, key_rope], -1)
    logits = jnp.einsum("shd,thd->hst", queries, keys_all, preferred_element_type=jnp.float32)
    logits = logits * HEAD ** (-0.5)
    allowed = (segments[:, None] == segments[None, :]) & (positions[None, :] <= positions[:, None])
    return jnp.max(jnp.where(allowed[None], logits, NEG), axis=(1, 2))


def scale_weights(own_max, q_weight, k_weight):
    factor = clip_threshold / jnp.maximum(own_max, clip_threshold)
    square_root = jnp.sqrt(factor)
    layers, heads = own_max.shape
    q_columns = jnp.concatenate(
        [
            jnp.broadcast_to(square_root[..., None], (layers, heads, NOPE)),
            jnp.broadcast_to(factor[..., None], (layers, heads, ROPE)),
        ],
        -1,
    ).reshape(layers, 1, heads * HEAD)
    k_columns = jnp.broadcast_to(square_root[..., None], (layers, heads, NOPE)).reshape(
        layers, 1, heads * NOPE
    )
    scaled_q = (q_weight.astype(jnp.float32) * q_columns).astype(jnp.bfloat16)
    scaled_k = (k_weight.astype(jnp.float32) * k_columns).astype(jnp.bfloat16)
    return scaled_q, scaled_k


def gathered_maxima(q_latent, kv_latent, segment_ids, q_weight, k_weight):
    q_full = jnp.dot(
        q_latent[0],
        lax.all_gather(q_weight[0], "dp", axis=0, tiled=True),
        preferred_element_type=jnp.float32,
    )
    own_max = sequence_maxima(q_full, kv_latent[0], segment_ids, k_weight[0])[None]
    layer_max = lax.pmax(own_max, "dp")
    return layer_max, lax.all_gather(layer_max, "section", axis=0, tiled=True)


def rope_tables(length):
    half = ROPE // 2
    frequency = np.float32(rope_base) ** (-np.arange(half, dtype=np.float32) / np.float32(half))
    angles = np.arange(length, dtype=np.float32)[:, None] * frequency[None, :].astype(np.float32)
    cosine, sine = np.cos(angles), np.sin(angles)
    zero = np.zeros_like(cosine)
    rest = np.zeros((length, ROPE), np.float32)
    low = [
        np.concatenate([cosine, cosine, rest + 1], 1),
        np.concatenate([-sine, zero, rest], 1),
        np.concatenate([zero, sine, rest], 1),
    ]
    high = [np.roll(t, ROPE, 1) for t in low]
    return np.stack(low + high).astype(np.float32)


def maxima_kernel(
    n_sec, lat_hbm, q_hbm, k_hbm, tab_ref, out_ref,
    lat, wq, wk, keys, bias, macc, tbuf,
    lat_recv, lat_send, w_recv, w_send, k_recv, k_send, t_recv, t_send,
):
    n_seq, length, _ = lat.shape
    rows = q_hbm.shape[0]
    n_pair, d_q, pair = wq.shape
    group_q, group_k = n_pair * pair, wk.shape[1]
    part = length // 2

    z, sec, y = lax.axis_index("dp"), lax.axis_index("section"), lax.axis_index("head")
    c = lax.rem(sec, 2)
    half, z_low = z // 2, lax.rem(z, 2)
    base = sec - c
    primary = c == half
    core_peer = {"section": base + 1 - c}
    y_peer = {"head": 1 - y}
    z_peer = {"dp": 2 * half + 1 - z_low}
    entry = jnp.where(half == 0, 1, 2)
    far = 2 * (1 - half)
    me = z * n_sec + sec

    barrier = pltpu.get_barrier_semaphore()
    for step in range(1, n_seq * n_sec):
        other = lax.rem(me + step, n_seq * n_sec)
        pl.semaphore_signal(
            barrier, inc=1, device_id={"dp": other // n_sec, "section": lax.rem(other, n_sec)},
            device_id_type=MESH,
        )
    pl.semaphore_signal(barrier, inc=1, device_id=y_peer, device_id_type=MESH)

    def local(src, dst, sem):
        return pltpu.make_async_copy(src, dst, sem)

    def ready(dst, sem):
        pltpu.make_async_copy(dst, dst, sem).wait()

    def remote(src, dst, send, recv, where):
        return pltpu.make_async_remote_copy(
            src_ref=src, dst_ref=dst, send_sem=send, recv_sem=recv,
            device_id=where, device_id_type=MESH,
        )

    def lat_at(seq, h):
        return lat.at[seq, pl.ds(h * part, part), :]

    def own_rows(h):
        return lat_hbm.at[pl.ds(h * part, part), :]

    pl.semaphore_wait(barrier, n_seq * n_sec)

    cross_send = remote(own_rows(y), lat_at(z, y), lat_send.at[0], lat_recv.at[z, y], {"dp": 3 - entry})
    near_send = remote(own_rows(y), lat_at(z, y), lat_send.at[0], lat_recv.at[z, y], z_peer)
    core_own = [
        remote(own_rows(h), lat_at(z, h), lat_send.at[1 + h], lat_recv.at[z, h], core_peer)
        for h in range(2)
    ]
    own_group = 2 * z_low + c
    peer_group = 2 * z_low + 1 - c
    k_own = local(k_hbm.at[:, pl.ds(own_group * group_k, group_k)], wk, k_recv)
    k_peer = remote(
        k_hbm.at[:, pl.ds(peer_group * group_k, group_k)], wk, k_send, k_recv, core_peer
    )

    @pl.when(jnp.logical_not(primary))
    def _():
        cross_send.start()

    @pl.when(primary)
    def _():
        near_send.start()
        for h in range(2):
            local(own_rows(h), lat_at(z, h), lat_recv.at[z, h]).start()
            core_own[h].start()
        k_own.start()
        k_peer.start()

    def send_columns(p):
        for j in range(4):
            z_to, c_to = 2 * c + j // 2, j % 2
            src = q_hbm.at[:, pl.ds(j * group_q + p * pair, pair)]
            dst = wq.at[p, pl.ds(z * rows, rows), :]
            mine = (z_to == z) & (c_to == c)

            @pl.when(mine)
            def _():
                local(src, dst, w_recv.at[p, z]).start()

            @pl.when(jnp.logical_not(mine))
            def _():
                remote(
                    src, dst, w_send.at[p, j], w_recv.at[p, z],
                    {"dp": z_to, "section": base + c_to},
                ).start()

    send_columns(0)
    send_columns(1)

    others = [2 * half + 1 - z_low, jnp.where(half == 0, 2, 1), jnp.where(half == 0, 3, 0)]

    def relay(i, seq, h, to_y, to_z):
        slot = lat_at(seq, h)
        sem = lat_recv.at[seq, h]
        out = [remote(slot, slot, lat_send.at[3 + 4 * i + (0 if to_y else 1)], sem, core_peer)]
        if to_y:
            out.append(remote(slot, slot, lat_send.at[3 + 4 * i + 2], sem, y_peer))
        return out, remote(slot, slot, lat_send.at[3 + 4 * i + 3], sem, z_peer)

    at_entry = z == entry

    @pl.when(primary)
    def _():
        for i, seq in enumerate(others):
            first, to_z = relay(i, seq, y, True, i > 0)
            ready(lat_at(seq, y), lat_recv.at[seq, y])
            if i > 0:
                @pl.when(at_entry)
                def _():
                    to_z.start()
            for copy in reversed(first):
                copy.start()
        for i, seq in enumerate(others):
            second, _ = relay(i, seq, 1 - y, False, False)
            ready(lat_at(seq, 1 - y), lat_recv.at[seq, 1 - y])
            second[0].start()
        for h in range(2):
            ready(lat_at(z, h), lat_recv.at[z, h])

    send_columns(2)
    send_columns(3)

    @pl.when(jnp.logical_not(primary))
    def _():
        for seq in range(n_seq):
            for h in range(2):
                ready(lat_at(seq, h), lat_recv.at[seq, h])

    ready(wk, k_recv)

    macc[...] = jnp.full(macc.shape, NEG, jnp.float32)
    lane = lax.broadcasted_iota(jnp.int32, (length, LANES), 1)
    low_lanes = lane < ROPE

    def seq_keys(s, carry):
        tail = lat[s, :, d_q + D_KV:].astype(jnp.float32)
        seg_row = tail.T[ROPE:ROPE + 1, :]
        seg_col = tail[:, ROPE:ROPE + 1]
        row = lax.broadcasted_iota(jnp.int32, (length, length), 0)
        col = lax.broadcasted_iota(jnp.int32, (length, length), 1)
        bias[s] = jnp.where((seg_col == seg_row) & (col <= row), 0.0, NEG)
        rope_low = jnp.where(low_lanes, tail, 0.0)
        rope_high = pltpu.roll(rope_low, ROPE, 1)

        def pair_keys(p, inner):
            columns = pl.ds(pl.multiple_of(p * 2 * NOPE, 2 * NOPE), 2 * NOPE)
            k2 = jnp.dot(
                lat[s, :, d_q:d_q + D_KV], wk[:, columns], preferred_element_type=jnp.float32
            )
            turned = pltpu.roll(k2[:, NOPE:], ROPE, 1)
            keys[s, p, 0, :, :NOPE] = k2[:, :NOPE].astype(jnp.bfloat16)
            keys[s, p, 0, :, NOPE:] = rope_low.astype(jnp.bfloat16)
            keys[s, p, 1, :, :NOPE] = jnp.where(low_lanes, 0.0, turned).astype(jnp.bfloat16)
            keys[s, p, 1, :, NOPE:] = jnp.where(low_lanes, turned, rope_high).astype(jnp.bfloat16)
            return inner

        return lax.fori_loop(0, n_pair, pair_keys, carry)

    lax.fori_loop(0, n_seq, seq_keys, 0)

    def turn(values, at):
        return (
            values * tab_ref[at]
            + pltpu.roll(values, LANES - ROPE // 2, 1) * tab_ref[at + 1]
            + pltpu.roll(values, ROPE // 2, 1) * tab_ref[at + 2]
        ).astype(jnp.bfloat16)

    def pair_logits(p, carry):
        for source in range(n_seq):
            ready(wq.at[p, pl.ds(source * rows, rows), :], w_recv.at[p, source])

        def one(s, inner):
            q2 = jnp.dot(lat[s, :, :d_q], wq[p], preferred_element_type=jnp.float32)
            first = q2[:, :NOPE].astype(jnp.bfloat16)
            middle = turn(q2[:, NOPE:2 * NOPE], 0)
            last = turn(q2[:, 2 * NOPE:], 3)
            for e, tiles in enumerate(((first, middle), (middle, last))):
                queries = jnp.concatenate(tiles, 1)
                for block in range(2):
                    lo, hi = block * part, (block + 1) * part
                    logits = lax.dot_general(
                        queries[lo:hi], keys[s, p, e, :hi, :], (((1,), (1,)), ((), ())),
                        preferred_element_type=jnp.float32,
                    ) + bias[s, lo:hi, :hi]
                    top = jnp.max(logits.reshape(part // 8, 8, hi), axis=0)
                    macc[2 * p + e, :, :hi] = jnp.maximum(macc[2 * p + e, :, :hi], top)
            return inner

        return lax.fori_loop(0, n_seq, one, carry)

    lax.fori_loop(0, n_pair, pair_logits, 0)

    top = jnp.max(jnp.max(macc[...], axis=1), axis=1, keepdims=True) * HEAD ** (-0.5)
    tile = jnp.broadcast_to(top, tbuf.shape)
    tbuf[...] = tile
    out_ref[me] = tile

    def sent(src, sem):
        pltpu.make_async_copy(src, src, sem).wait()

    for p in range(n_pair):
        for j in range(4):
            mine = (2 * c + j // 2 == z) & (j % 2 == c)

            @pl.when(jnp.logical_not(mine))
            def _():
                sent(q_hbm.at[:, pl.ds(j * group_q + p * pair, pair)], w_send.at[p, j])

    @pl.when(jnp.logical_not(primary))
    def _():
        cross_send.wait_send()

    @pl.when(primary)
    def _():
        near_send.wait_send()
        for h in range(2):
            core_own[h].wait_send()
        k_peer.wait_send()
        for i, seq in enumerate(others):
            first, to_z = relay(i, seq, y, True, i > 0)
            for copy in first:
                copy.wait_send()
            if i > 0:
                @pl.when(at_entry)
                def _():
                    to_z.wait_send()
            second, _ = relay(i, seq, 1 - y, False, False)
            second[0].wait_send()

    def table_copy(step):
        other = lax.rem(me + step, n_seq * n_sec)
        return remote(
            tbuf, out_ref.at[me], t_send.at[step], t_recv.at[me],
            {"dp": other // n_sec, "section": lax.rem(other, n_sec)},
        )

    for step in range(1, n_seq * n_sec):
        table_copy(step).start()
    for step in range(1, n_seq * n_sec):
        source = lax.rem(me + step, n_seq * n_sec)
        ready(out_ref.at[source], t_recv.at[source])
    for step in range(1, n_seq * n_sec):
        table_copy(step).wait_send()


def exchanged_maxima(sizes, q_latent, kv_latent, segment_ids, q_weight, k_weight):
    n_dp, n_sec = sizes
    _, length, d_q = q_latent.shape
    rows = q_weight.shape[1]
    heads = k_weight.shape[2] // NOPE
    group = heads // n_dp
    n_pair = group // 2
    width = d_q + D_KV + LANES
    lat = jnp.concatenate(
        [
            q_latent[0],
            kv_latent[0],
            segment_ids[:, None].astype(jnp.bfloat16),
            jnp.zeros((length, LANES - ROPE - 1), jnp.bfloat16),
        ],
        1,
    )
    bf16, dma = jnp.bfloat16, pltpu.SemaphoreType.DMA
    n_all = n_dp * n_sec
    table = pl.pallas_call(
        functools.partial(maxima_kernel, n_sec),
        out_shape=jax.ShapeDtypeStruct((n_all, group, LANES), jnp.float32),
        in_specs=[pl.BlockSpec(memory_space=pltpu.HBM)] * 3
        + [pl.BlockSpec(memory_space=pltpu.VMEM)],
        out_specs=pl.BlockSpec(memory_space=pltpu.VMEM),
        scratch_shapes=[
            pltpu.VMEM((n_dp, length, width), bf16),
            pltpu.VMEM((n_pair, d_q, 2 * HEAD), bf16),
            pltpu.VMEM((D_KV, group * NOPE), bf16),
            pltpu.VMEM((n_dp, n_pair, 2, length, 2 * NOPE), bf16),
            pltpu.VMEM((n_dp, length, length), jnp.float32),
            pltpu.VMEM((group, 8, length), jnp.float32),
            pltpu.VMEM((group, LANES), jnp.float32),
            dma((n_dp, 2)),
            dma((15,)),
            dma((n_pair, n_dp)),
            dma((n_pair, 4)),
            dma,
            dma,
            dma((n_all,)),
            dma((n_all,)),
        ],
        compiler_params=pltpu.CompilerParams(
            collective_id=0, has_side_effects=True, vmem_limit_bytes=60 * 1024 * 1024
        ),
        name="maxima",
    )(lat, q_weight[0], k_weight[0], jnp.asarray(rope_tables(length)))
    by_device = table[:, :, 0].reshape(2, n_dp // 2, n_sec // 2, 2, group)
    max_table = by_device.transpose(2, 0, 1, 3, 4).reshape(n_sec, heads)
    own = lax.dynamic_slice_in_dim(max_table, lax.axis_index("section"), 1, 0)
    return own, max_table


def per_device(sizes, q_latent, kv_latent, segment_ids, q_weight, k_weight):
    n_dp, n_sec, n_head = sizes
    heads = k_weight.shape[2] // NOPE
    length = q_latent.shape[1]
    exchange = (
        n_dp == 4 and n_sec % 2 == 0 and n_head == 2 and heads == 8 * n_dp
        and length % 512 == 0 and q_latent.shape[0] == 1
    )
    args = (q_latent, kv_latent, segment_ids, q_weight, k_weight)
    if exchange:
        own, max_table = exchanged_maxima((n_dp, n_sec), *args)
    else:
        own, max_table = gathered_maxima(*args)
    scaled_q, scaled_k = scale_weights(own, q_weight, k_weight)
    return max_table / clip_threshold, scaled_q, scaled_k


def solution(mesh):
    sizes = tuple(mesh.shape[axis] for axis in ("dp", "section", "head"))
    return jax.shard_map(
        functools.partial(per_device, sizes),
        mesh=mesh,
        in_specs=(
            P("section", "dp", None),
            P("section", "dp", None),
            P("dp"),
            P("section", "dp", "head"),
            P("section", None, "head"),
        ),
        out_specs=(P(None, "head"), P("section", "dp", "head"), P("section", None, "head")),
        check_vma=False,
    )
```

time: 419 us -> 163 us (0.39)
  waiting for transfers between devices: 313 us -> 0 us
  Pallas kernels: 0 us -> 145 us
  local copies, waits for them, and re-layouts: 36.6 us -> 7.24 us
  matrix products: 29.2 us -> 0 us
  blocking collectives: 14.5 us -> 0 us
  between operations: 14.1 us -> 0.69 us
    all_gather x1 -> x0, waiting for transfers between devices: 312 us -> none  [per_device(): lax.all_gather(q_weight[0], 'dp', axis=0, tiled=True)]
    pallas_call x0 -> x1, Pallas kernels: none -> 145 us  [exchanged_maxima(): pl.pallas_call(functools.partial(maxima_kernel, n_sec), out_shape=jax.Sha...]
    dot_general x3 -> x0, matrix products: 29.2 us -> none  [the longest x1 14.1 us: per_device(): jnp.dot(latent_q, lax.all_gather(q_weight[0], 'dp', axis=0, tiled=True),...]
    dot_general x1 -> x0, local copies, waits for them, and re-layouts: 24.6 us -> none  [per_device(): jnp.dot(latent_q, lax.all_gather(q_weight[0], 'dp', axis=0, tiled=True),...]
    pmax x1 -> x0, blocking collectives: 9.41 us -> none  [per_device(): layer_max = lax.pmax(own_max, 'dp')]
    reshape x1, local copies, waits for them, and re-layouts: 6.55 us -> 0.09 us  [exchanged_maxima(): max_table = by_device.transpose(2, 0, 1, 3, 4).reshape(n_sec, heads)]
    all_gather x1 -> x0, blocking collectives: 5.06 us -> none  [per_device(): max_table = lax.all_gather(layer_max, 'section', axis=0, tiled=True)]
    concatenate x0 -> x1, local copies, waits for them, and re-layouts: none -> 4.4 us  [exchanged_maxima(): jnp.concatenate([q_latent[0], kv_latent[0], segment_ids[:, None].astype(j...]
  transfers between devices with their start and end apart: 1 -> 0, of which waited for: 1 -> 0; matrix products, arithmetic and copies ran while one was open for 4% -> 0% of each run, Pallas kernels for 0% -> 0%
where the time goes in v1:
time: 163 us
  Pallas kernels  145 us (89%)
  other arithmetic  10 us (6%)
  local copies, waits for them, and re-layouts  7.24 us (4%)
    pallas_call x1, Pallas kernels, exchanged_maxima(): pl.pallas_call(functools.partial(maxima_kernel, n_sec), out_shape=jax.Sha...  145 us
    convert_element_type x1, other arithmetic, scale_weights(): scaled_q = (q_weight.astype(jnp.float32) * q_columns).astype(jnp.bfloat16)  5.84 us
    concatenate x1, local copies, waits for them, and re-layouts, exchanged_maxima(): jnp.concatenate([q_latent[0], kv_latent[0], segment_ids[:, None].astype(j...  4.4 us

profile of v1, /device:TPU:0, one launch (start us, length us, event | category | flops | bytes accessed | tf_op | source)
XLA Modules:
  0.0 162.8 jit_solution(1954902701902941861)
XLA Ops:
  0.6 1.4 copy.11
  2.0 0.7 convert_element_type.18
  2.7 0.1 convert_element_type.24
  2.8 4.4 %concatenate.6.lat_hbm = bf16[512,2176]{1,0:T(8,128)(2,1)} concatenate(bf16[512,1536]{1,0:T(8,128)(2,1)} %bitcast.15, bf16[512,576]{1,0:T(8,128)(2,1)S(1)} %bitcast.14, bf16[512,1]{1,0:T(8,128)(2,1)S(1)} %convert_element_type.24, bf16[512,63]{1,0:T(8,128)(2,1)S(1)} %broadcast_in_dim.28), dimensions={1} | concatenate | bytes 4456448 | tf_op jit(solution)/shard_map/concatenate | solution.py:368
  7.3 144.8 %maxima.1 = f32[16,8,128]{2,1,0:T(8,128)} custom-call(bf16[512,2176]{1,0:T(8,128)(2,1)} %concatenate.6.lat_hbm, bf16[384,6144]{1,0:T(8,128)(2,1)} %bitcast.12, bf16[512,4096]{1,0:T(8,128)(2,1)} %bitcast.13, f32[6,512,128]{2,1,0:T(8,128)} %constant.19.clone.tab_ref), custom_call_target="tpu_custom_call" | custom-call | tf_op jit(solution)/shard_map/maxima/pallas_call | solution.py:379
  152.1 0.9 slice_reduce_fusion
  153.0 0.1 reshape.26
  153.1 0.1 broadcast_in_dim.30
  153.2 0.1 broadcast_in_dim.32
  153.3 0.1 mul.18
  153.4 0.0 copy-start
  153.4 5.8 %multiply_convert_fusion = bf16[1,384,6144]{2,1,0:T(8,128)(2,1)} fusion(bf16[1,384,6144]{2,1,0:T(8,128)(2,1)} %param.9, f32[6144]{0:T(1024)S(1)} %mul.18), kind=kLoop, calls=%fused_computation | loop fusion | flops 7077888 | bytes 9461760 | tf_op jit(solution)/shard_map/convert_element_type | solution.py:73
  159.2 0.1 broadcast_bitcast_fusion
  159.3 0.0 copy-done
  159.3 2.9 %multiply_convert_fusion.1 = bf16[1,512,4096]{2,1,0:T(8,128)(2,1)} fusion(bf16[1,512,4096]{2,1,0:T(8,128)(2,1)S(1)} %copy-done, f32[4096]{0:T(1024)S(1)} %broadcast_bitcast_fusion), kind=kLoop, calls=%fused_computation.1 | loop fusion | flops 6291456 | bytes 8404992 | tf_op jit(solution)/shard_map/convert_element_type | solution.py:74
  162.2 0.6 broadcast_multiply_fusion
  (4 shorter events, 0.0 us)
Async XLA Ops:
  153.4 5.9 %copy-start = (bf16[1,512,4096]{2,1,0:T(8,128)(2,1)S(1)}, bf16[1,512,4096]{2,1,0:T(8,128)(2,1)}, u32[]{:S(2)}) copy-start(bf16[1,512,4096]{2,1,0:T(8,128)(2,1)} %param.10) | copy-start | bytes 12582916

commit v2 on v1

v2 whole, which is shorter than its diff:
```python
import functools
import jax
import jax.numpy as jnp
import numpy as np
from jax import lax
from jax.experimental import pallas as pl
from jax.experimental.pallas import tpu as pltpu
from jax.sharding import PartitionSpec as P

D_KV = 512
NOPE = 128
ROPE = 64
HEAD = NOPE + ROPE
LANES = 128
NEG = -1e30
VMEM_MIB = 44
MESH = pl.DeviceIdType.MESH

clip_threshold = 100.0
rope_base = 50000.0


def rotate(values, positions):
    half_width = values.shape[-1] // 2
    frequency = rope_base ** (-jnp.arange(half_width, dtype=jnp.float32) / half_width)
    angles = positions[:, None].astype(jnp.float32) * frequency[None, :]
    cosine = jnp.cos(angles)[:, None, :]
    sine_part = jnp.sin(angles)[:, None, :]
    lower_half = values[..., :half_width]
    upper_half = values[..., half_width:]
    return jnp.concatenate(
        [
            lower_half * cosine - upper_half * sine_part,
            upper_half * cosine + lower_half * sine_part,
        ],
        -1,
    )


def sequence_maxima(q_full, kv_rows, segments, w_key):
    length = kv_rows.shape[0]
    heads_here = w_key.shape[1] // NOPE
    q_full = q_full.reshape(length, heads_here, HEAD)
    positions = jnp.arange(length, dtype=jnp.int32)
    queries = jnp.concatenate(
        [q_full[..., :NOPE], rotate(q_full[..., NOPE:], positions)], -1
    ).astype(jnp.bfloat16)
    key_nope = jnp.dot(kv_rows[:, :D_KV], w_key, preferred_element_type=jnp.float32).astype(
        jnp.bfloat16
    )
    key_nope = key_nope.reshape(length, heads_here, NOPE)
    key_rope = jnp.broadcast_to(kv_rows[:, None, D_KV:], (length, heads_here, ROPE))
    keys_all = jnp.concatenate([key_nope, key_rope], -1)
    logits = jnp.einsum("shd,thd->hst", queries, keys_all, preferred_element_type=jnp.float32)
    logits = logits * HEAD ** (-0.5)
    allowed = (segments[:, None] == segments[None, :]) & (positions[None, :] <= positions[:, None])
    return jnp.max(jnp.where(allowed[None], logits, NEG), axis=(1, 2))


def scale_weights(own_max, q_weight, k_weight):
    factor = clip_threshold / jnp.maximum(own_max, clip_threshold)
    square_root = jnp.sqrt(factor)
    layers, heads = own_max.shape
    q_columns = jnp.concatenate(
        [
            jnp.broadcast_to(square_root[..., None], (layers, heads, NOPE)),
            jnp.broadcast_to(factor[..., None], (layers, heads, ROPE)),
        ],
        -1,
    ).reshape(layers, 1, heads * HEAD)
    k_columns = jnp.broadcast_to(square_root[..., None], (layers, heads, NOPE)).reshape(
        layers, 1, heads * NOPE
    )
    scaled_q = (q_weight.astype(jnp.float32) * q_columns).astype(jnp.bfloat16)
    scaled_k = (k_weight.astype(jnp.float32) * k_columns).astype(jnp.bfloat16)
    return scaled_q, scaled_k


def gathered_maxima(q_latent, kv_latent, segment_ids, q_weight, k_weight):
    q_full = jnp.dot(
        q_latent[0],
        lax.all_gather(q_weight[0], "dp", axis=0, tiled=True),
        preferred_element_type=jnp.float32,
    )
    own_max = sequence_maxima(q_full, kv_latent[0], segment_ids, k_weight[0])[None]
    layer_max = lax.pmax(own_max, "dp")
    return layer_max, lax.all_gather(layer_max, "section", axis=0, tiled=True)


def rope_tables(length):
    half = ROPE // 2
    frequency = np.float32(rope_base) ** (-np.arange(half, dtype=np.float32) / np.float32(half))
    angles = np.arange(length, dtype=np.float32)[:, None] * frequency[None, :].astype(np.float32)
    cosine, sine = np.cos(angles), np.sin(angles)
    zero = np.zeros_like(cosine)
    rest = np.zeros((length, ROPE), np.float32)
    low = [
        np.concatenate([cosine, cosine, rest + 1], 1),
        np.concatenate([-sine, zero, rest], 1),
        np.concatenate([zero, sine, rest], 1),
    ]
    high = [np.roll(t, ROPE, 1) for t in low]
    return np.stack(low + high).astype(np.float32)


def maxima_kernel(
    n_sec, x_hbm, kv_hbm, seg_hbm, q_hbm, k_hbm, tab_ref, out_ref,
    lat, kvt, seg, wq, wk, keys, bias, macc, tbuf,
    lat_recv, lat_send, seg_recv, seg_send, w_recv, w_send, k_recv, k_send, t_recv, t_send,
):
    n_seq, length, _ = lat.shape
    rows = q_hbm.shape[0]
    n_pair, d_q, pair = wq.shape
    group_q, group_k = n_pair * pair, wk.shape[1]
    part = length // 2

    z, sec, y = lax.axis_index("dp"), lax.axis_index("section"), lax.axis_index("head")
    c = lax.rem(sec, 2)
    half, z_low = z // 2, lax.rem(z, 2)
    base = sec - c
    primary = c == half
    core_peer = {"section": base + 1 - c}
    y_peer = {"head": 1 - y}
    z_peer = {"dp": 2 * half + 1 - z_low}
    entry = jnp.where(half == 0, 1, 2)
    me = z * n_sec + sec

    barrier = pltpu.get_barrier_semaphore()
    for step in range(1, n_seq * n_sec):
        other = lax.rem(me + step, n_seq * n_sec)
        pl.semaphore_signal(
            barrier, inc=1, device_id={"dp": other // n_sec, "section": lax.rem(other, n_sec)},
            device_id_type=MESH,
        )
    pl.semaphore_signal(barrier, inc=1, device_id=y_peer, device_id_type=MESH)

    def local(src, dst, sem):
        return pltpu.make_async_copy(src, dst, sem)

    def ready(dst, sem):
        pltpu.make_async_copy(dst, dst, sem).wait()

    def remote(src, dst, send, recv, where):
        return pltpu.make_async_remote_copy(
            src_ref=src, dst_ref=dst, send_sem=send, recv_sem=recv,
            device_id=where, device_id_type=MESH,
        )

    def slots(seq, h):
        at = pl.ds(pl.multiple_of(h * part, part), part)
        return lat.at[seq, at, :], kvt.at[seq, :, at]

    def own(h):
        at = pl.ds(pl.multiple_of(h * part, part), part)
        return x_hbm.at[at, :], kv_hbm.at[:, at]

    def send(sources, seq, h, at, where, do):
        for i, (src, dst) in enumerate(zip(sources, slots(seq, h))):
            getattr(
                remote(src, dst, lat_send.at[at, i], lat_recv.at[seq, h, i], where), do
            )()

    def ready_half(seq, h):
        for i, dst in enumerate(slots(seq, h)):
            ready(dst, lat_recv.at[seq, h, i])

    own_group = 2 * z_low + c
    peer_group = 2 * z_low + 1 - c

    def group_columns(g):
        return k_hbm.at[:, pl.ds(pl.multiple_of(g * group_k, group_k), group_k)]

    def seg_copy(step):
        return remote(
            seg_hbm, seg.at[z], seg_send.at[step], seg_recv.at[z],
            {"dp": lax.rem(z + step, n_seq)},
        )

    def own_sends(do):
        for step in range(1, n_seq):
            getattr(seg_copy(step), do)()

        @pl.when(jnp.logical_not(primary))
        def _():
            send(own(y), z, y, 0, {"dp": 3 - entry}, do)

        @pl.when(primary)
        def _():
            send(own(y), z, y, 0, z_peer, do)
            for h in range(2):
                send(own(h), z, h, 1 + h, core_peer, do)
            k_peer = remote(group_columns(peer_group), wk, k_send, k_recv, core_peer)
            getattr(k_peer, do)()

    def columns(p, j, act):
        turn_to = lax.rem(j + 2 * z_low, 4)
        z_to, c_to = 2 * c + turn_to // 2, lax.rem(turn_to, 2)
        offset = pl.multiple_of(turn_to * group_q + p * pair, LANES)
        src = q_hbm.at[:, pl.ds(offset, pair)]
        dst = wq.at[p, pl.ds(pl.multiple_of(z * rows, rows), rows), :]
        mine = (z_to == z) & (c_to == c)
        there = {"dp": z_to, "section": base + c_to}
        if act == "start":
            @pl.when(mine)
            def _():
                local(src, dst, w_recv.at[p, z]).start()

        @pl.when(jnp.logical_not(mine))
        def _():
            getattr(remote(src, dst, w_send.at[p, j], w_recv.at[p, z], there), act)()

    def send_columns(p):
        for j in range(4):
            columns(p, j, "start")

    pl.semaphore_wait(barrier, n_seq * n_sec)

    own_sends("start")
    local(seg_hbm, seg.at[z], seg_recv.at[z]).start()

    @pl.when(primary)
    def _():
        for h in range(2):
            for i, (src, dst) in enumerate(zip(own(h), slots(z, h))):
                local(src, dst, lat_recv.at[z, h, i]).start()
        local(group_columns(own_group), wk, k_recv).start()

    send_columns(0)
    send_columns(1)

    others = [2 * half + 1 - z_low, jnp.where(half == 0, 2, 1), jnp.where(half == 0, 3, 0)]
    at_entry = z == entry

    def relay_first(i, seq, do):
        if i > 0:
            @pl.when(at_entry)
            def _():
                send(slots(seq, y), seq, y, 6 + 4 * i, z_peer, do)
        send(slots(seq, y), seq, y, 5 + 4 * i, y_peer, do)
        send(slots(seq, y), seq, y, 3 + 4 * i, core_peer, do)

    def relay_second(i, seq, do):
        send(slots(seq, 1 - y), seq, 1 - y, 4 + 4 * i, core_peer, do)

    @pl.when(primary)
    def _():
        for i, seq in enumerate(others):
            ready_half(seq, y)
            relay_first(i, seq, "start")
        for i, seq in enumerate(others):
            ready_half(seq, 1 - y)
            relay_second(i, seq, "start")
        for h in range(2):
            ready_half(z, h)

    send_columns(2)
    send_columns(3)

    @pl.when(jnp.logical_not(primary))
    def _():
        for seq in range(n_seq):
            for h in range(2):
                ready_half(seq, h)

    ready(wk, k_recv)
    for seq in range(n_seq):
        ready(seg.at[seq], seg_recv.at[seq])

    macc[...] = jnp.full(macc.shape, NEG, jnp.float32)

    def seq_keys(s, carry):
        seg_row = seg[s].astype(jnp.float32)
        seg_col = jnp.broadcast_to(seg_row, (LANES, length)).T[:, :1]
        row = lax.broadcasted_iota(jnp.int32, (length, length), 0)
        col = lax.broadcasted_iota(jnp.int32, (length, length), 1)
        bias[s] = jnp.where((seg_col == seg_row) & (col <= row), 0.0, NEG)
        rope = kvt[s, D_KV:, :]
        none = jnp.zeros((ROPE, length), jnp.bfloat16)
        for p in range(n_pair):
            k2 = lax.dot_general(
                wk[:, p * 2 * NOPE:(p + 1) * 2 * NOPE], kvt[s, :D_KV, :],
                (((0,), (0,)), ((), ())), preferred_element_type=jnp.float32,
            ).astype(jnp.bfloat16)
            keys[s, p, 0, :NOPE, :] = k2[:NOPE]
            keys[s, p, 0, NOPE:HEAD, :] = rope
            keys[s, p, 0, HEAD:, :] = none
            keys[s, p, 1, :ROPE, :] = none
            keys[s, p, 1, ROPE:HEAD, :] = k2[NOPE:]
            keys[s, p, 1, HEAD:, :] = rope
        return carry

    lax.fori_loop(0, n_seq, seq_keys, 0)

    def turn(values, at):
        return (
            values * tab_ref[at]
            + pltpu.roll(values, LANES - ROPE // 2, 1) * tab_ref[at + 1]
            + pltpu.roll(values, ROPE // 2, 1) * tab_ref[at + 2]
        ).astype(jnp.bfloat16)

    def pair_logits(p, carry):
        for source in range(n_seq):
            ready(wq.at[p, pl.ds(source * rows, rows), :], w_recv.at[p, source])

        def one(s, inner):
            q2 = jnp.dot(lat[s], wq[p], preferred_element_type=jnp.float32)
            first = q2[:, :NOPE].astype(jnp.bfloat16)
            middle = turn(q2[:, NOPE:2 * NOPE], 0)
            last = turn(q2[:, 2 * NOPE:], 3)
            for e, tiles in enumerate(((first, middle), (middle, last))):
                queries = jnp.concatenate(tiles, 1)
                for block in range(2):
                    lo, hi = block * part, (block + 1) * part
                    logits = jnp.dot(
                        queries[lo:hi], keys[s, p, e, :, :hi], preferred_element_type=jnp.float32
                    ) + bias[s, lo:hi, :hi]
                    top = jnp.max(logits.reshape(part // 8, 8, hi), axis=0)
                    macc[2 * p + e, :, :hi] = jnp.maximum(macc[2 * p + e, :, :hi], top)
            return inner

        return lax.fori_loop(0, n_seq, one, carry)

    lax.fori_loop(0, n_pair, pair_logits, 0)

    top = jnp.max(jnp.max(macc[...], axis=1), axis=1, keepdims=True) * HEAD ** (-0.5)
    tile = jnp.broadcast_to(top, tbuf.shape)
    tbuf[...] = tile
    out_ref[me] = tile

    for p in range(n_pair):
        for j in range(4):
            columns(p, j, "wait_send")
    own_sends("wait_send")

    @pl.when(primary)
    def _():
        for i, seq in enumerate(others):
            relay_first(i, seq, "wait_send")
            relay_second(i, seq, "wait_send")

    def table_copy(step):
        other = lax.rem(me + step, n_seq * n_sec)
        return remote(
            tbuf, out_ref.at[me], t_send.at[step], t_recv.at[me],
            {"dp": other // n_sec, "section": lax.rem(other, n_sec)},
        )

    for step in range(1, n_seq * n_sec):
        table_copy(step).start()
    for step in range(1, n_seq * n_sec):
        source = lax.rem(me + step, n_seq * n_sec)
        ready(out_ref.at[source], t_recv.at[source])
    for step in range(1, n_seq * n_sec):
        table_copy(step).wait_send()


def scale_kernel(n_sec, table, q_ref, k_ref, ratio_ref, q_out, k_out):
    n_group = pl.num_programs(0)
    g = pl.program_id(0)
    sec = lax.axis_index("section")
    group = table.shape[1]

    def slot(layer, number):
        z_of = 2 * lax.rem(layer, 2) + number // 2
        return z_of * n_sec + 2 * (layer // 2) + lax.rem(number, 2)

    factor = clip_threshold / jnp.maximum(table[slot(sec, g)], clip_threshold)
    root = jnp.sqrt(factor)
    low = lax.broadcasted_iota(jnp.int32, (1, LANES), 1) < ROPE
    for p in range(group // 2):
        f_a, f_b = factor[2 * p:2 * p + 1], factor[2 * p + 1:2 * p + 2]
        r_a, r_b = root[2 * p:2 * p + 1], root[2 * p + 1:2 * p + 2]
        scales = (r_a, jnp.where(low, f_a, r_b), jnp.where(low, r_b, f_b))
        for i, scale in enumerate(scales):
            at = pl.ds(p * 2 * HEAD + i * LANES, LANES)
            q_out[:, at] = (q_ref[:, at].astype(jnp.float32) * scale).astype(jnp.bfloat16)
        for i, scale in enumerate((r_a, r_b)):
            at = pl.ds((2 * p + i) * NOPE, NOPE)
            k_out[:, at] = (k_ref[:, at].astype(jnp.float32) * scale).astype(jnp.bfloat16)

    @pl.when(g == 0)
    def _():
        lane = lax.broadcasted_iota(jnp.int32, (group, LANES), 1)
        place = lax.broadcasted_iota(jnp.int32, (group, LANES), 0)
        for layer in range(ratio_ref.shape[0]):
            line = jnp.zeros((1, LANES), jnp.float32)
            for number in range(ratio_ref.shape[1] // group):
                z_of = 2 * (layer % 2) + number // 2
                values = table[z_of * n_sec + 2 * (layer // 2) + number % 2]
                here = lane == number * group + place
                line = line + jnp.sum(jnp.where(here, values, 0.0), axis=0, keepdims=True)
            ratio_ref[layer:layer + 1, :] = line[:, :ratio_ref.shape[1]] / clip_threshold


def exchanged(sizes, q_latent, kv_latent, segment_ids, q_weight, k_weight):
    n_dp, n_sec = sizes
    _, length, d_q = q_latent.shape
    rows = q_weight.shape[1]
    heads = k_weight.shape[2] // NOPE
    group = heads // n_dp
    n_pair = group // 2
    bf16, dma = jnp.bfloat16, pltpu.SemaphoreType.DMA
    n_all = n_dp * n_sec
    table = pl.pallas_call(
        functools.partial(maxima_kernel, n_sec),
        out_shape=jax.ShapeDtypeStruct((n_all, group, LANES), jnp.float32),
        in_specs=[pl.BlockSpec(memory_space=pltpu.HBM)] * 5
        + [pl.BlockSpec(memory_space=pltpu.VMEM)],
        out_specs=pl.BlockSpec(memory_space=pltpu.VMEM),
        scratch_shapes=[
            pltpu.VMEM((n_dp, length, d_q), bf16),
            pltpu.VMEM((n_dp, D_KV + ROPE, length), bf16),
            pltpu.VMEM((n_dp, 1, length), jnp.int32),
            pltpu.VMEM((n_pair, d_q, 2 * HEAD), bf16),
            pltpu.VMEM((D_KV, group * NOPE), bf16),
            pltpu.VMEM((n_dp, n_pair, 2, 2 * NOPE, length), bf16),
            pltpu.VMEM((n_dp, length, length), jnp.float32),
            pltpu.VMEM((group, 8, length), jnp.float32),
            pltpu.VMEM((group, LANES), jnp.float32),
            dma((n_dp, 2, 2)),
            dma((15, 2)),
            dma((n_dp,)),
            dma((n_dp,)),
            dma((n_pair, n_dp)),
            dma((n_pair, 4)),
            dma,
            dma,
            dma((n_all,)),
            dma((n_all,)),
        ],
        compiler_params=pltpu.CompilerParams(
            collective_id=0, has_side_effects=True, vmem_limit_bytes=VMEM_MIB * 1024 * 1024
        ),
        cost_estimate=pl.CostEstimate(
            flops=2 * n_dp * length * group * (HEAD * (d_q + length) + NOPE * D_KV),
            bytes_accessed=2 * rows * heads * HEAD, transcendentals=0,
        ),
        name="maxima",
    )(
        q_latent[0], kv_latent[0].T, segment_ids.reshape(1, length), q_weight[0], k_weight[0],
        jnp.asarray(rope_tables(length)),
    )
    ratio, scaled_q, scaled_k = pl.pallas_call(
        functools.partial(scale_kernel, n_sec),
        grid=(n_dp,),
        out_shape=(
            jax.ShapeDtypeStruct((n_sec, heads), jnp.float32),
            jax.ShapeDtypeStruct(q_weight.shape[1:], bf16),
            jax.ShapeDtypeStruct(k_weight.shape[1:], bf16),
        ),
        in_specs=[
            pl.BlockSpec((n_all, group, LANES), lambda g: (0, 0, 0)),
            pl.BlockSpec((rows, group * HEAD), lambda g: (0, g)),
            pl.BlockSpec((D_KV, group * NOPE), lambda g: (0, g)),
        ],
        out_specs=[
            pl.BlockSpec((n_sec, heads), lambda g: (0, 0)),
            pl.BlockSpec((rows, group * HEAD), lambda g: (0, g)),
            pl.BlockSpec((D_KV, group * NOPE), lambda g: (0, g)),
        ],
        compiler_params=pltpu.CompilerParams(
            dimension_semantics=("arbitrary",), vmem_limit_bytes=24 * 1024 * 1024
        ),
        cost_estimate=pl.CostEstimate(
            flops=rows * heads * HEAD, bytes_accessed=8 * rows * heads * HEAD, transcendentals=0
        ),
        name="scale",
    )(table, q_weight[0], k_weight[0])
    return ratio, scaled_q[None], scaled_k[None]


def per_device(sizes, q_latent, kv_latent, segment_ids, q_weight, k_weight):
    n_dp, n_sec, n_head = sizes
    heads = k_weight.shape[2] // NOPE
    length = q_latent.shape[1]
    exchange = (
        n_dp == 4 and n_sec % 2 == 0 and q_weight.shape[1] % 8 == 0 and n_head == 2 and heads == 8 * n_dp
        and length % 512 == 0 and q_latent.shape[0] == 1
    )
    args = (q_latent, kv_latent, segment_ids, q_weight, k_weight)
    if exchange:
        return exchanged((n_dp, n_sec), *args)
    own, max_table = gathered_maxima(*args)
    scaled_q, scaled_k = scale_weights(own, q_weight, k_weight)
    return max_table / clip_threshold, scaled_q, scaled_k


def solution(mesh):
    sizes = tuple(mesh.shape[axis] for axis in ("dp", "section", "head"))
    return jax.shard_map(
        functools.partial(per_device, sizes),
        mesh=mesh,
        in_specs=(
            P("section", "dp", None),
            P("section", "dp", None),
            P("dp"),
            P("section", "dp", "head"),
            P("section", None, "head"),
        ),
        out_specs=(P(None, "head"), P("section", "dp", "head"), P("section", None, "head")),
        check_vma=False,
    )
```

time: 163 us -> 154 us (0.945)
  other arithmetic: 10 us -> 0 us
  Pallas kernels: 145 us -> 147 us
    convert_element_type x3 -> x0, other arithmetic: 9.42 us -> none  [the longest x1 5.84 us: scale_weights(): scaled_q = (q_weight.astype(jnp.float32) * q_columns).astype(jnp.bfloat16)]
    unnamed x3 -> x12, local copies, waits for them, and re-layouts: 1.36 us -> 6.74 us
    concatenate x1 -> x0, local copies, waits for them, and re-layouts: 4.4 us -> none  [exchanged_maxima(): jnp.concatenate([q_latent[0], kv_latent[0], segment_ids[:, None].astype(j...]
    pallas_call x1 -> x2, Pallas kernels: 145 us -> 147 us  [the longest x1 142 us: exchanged(): pl.pallas_call(functools.partial(maxima_kernel, n_sec), out_shape=jax.Sha...]
where the time goes in v2:
time: 154 us
  Pallas kernels  147 us (95%)
  local copies, waits for them, and re-layouts  6.74 us (4%)
    pallas_call x1, Pallas kernels, exchanged(): pl.pallas_call(functools.partial(maxima_kernel, n_sec), out_shape=jax.Sha...  142 us
    unnamed x12, local copies, waits for them, and re-layouts  6.74 us
    pallas_call x1, Pallas kernels, exchanged(): pl.pallas_call(functools.partial(scale_kernel, n_sec), grid=(n_dp,), out_...  5.03 us

profile of v2, /device:TPU:0, one launch (start us, length us, event | category | flops | bytes accessed | tf_op | source)
XLA Modules:
  0.0 154.0 jit_solution(4173904107391167157)
XLA Ops:
  0.6 0.0 copy-start.1
  0.6 2.2 %copy-done.1 = bf16[1,512,4096]{2,1,0:T(8,128)(2,1)S(1)} copy-done((bf16[1,512,4096]{2,1,0:T(8,128)(2,1)S(1)}, bf16[1,512,4096]{2,1,0:T(8,128)(2,1)}, u32[]{:S(2)}) %copy-start.1) | copy-done | bytes 4194328
  2.8 0.0 copy-start.2
  2.8 1.4 copy-done.2
  4.2 0.0 copy-start.3
  4.2 1.1 copy-done.3
  5.3 0.0 copy-start.4
  5.3 0.7 copy-done.4
  6.0 0.0 copy-start.5
  6.0 1.4 copy-done.5
  7.4 0.0 copy-start
  7.4 141.6 %maxima.1.table = f32[16,8,128]{2,1,0:T(8,128)S(1)} custom-call(bf16[512,1536]{1,0:T(8,128)(2,1)S(1)} %bitcast.13, bf16[576,512]{1,0:T(8,128)(2,1)S(1)} %bitcast.14, s32[1,512]{1,0:T(1,128)S(1)} %bitcast.15, bf16[384,6144]{1,0:T(8,128)(2,1)} %bitcast.9, bf16[512,4096]{1,0:T(8,128)(2,1)S(1)} %bitcast.11, f32[6,512,128]{2,1,0:T(8,128)S(1)} %copy-done.5), custom_call_target="tpu_custom_call" | custom-call | flops 15032385536 | bytes 4718592 | tf_op jit(solution)/shard_map/maxima/pallas_call | solution.py:404
  148.9 0.0 copy-done
  149.0 5.0 %scale.1 = (f32[4,32]{1,0:T(4,128)}, bf16[384,6144]{1,0:T(8,128)(2,1)}, bf16[512,4096]{1,0:T(8,128)(2,1)}) custom-call(f32[16,8,128]{2,1,0:T(8,128)S(1)} %maxima.1.table, bf16[384,6144]{1,0:T(8,128)(2,1)S(1)} %bitcast.10, bf16[512,4096]{1,0:T(8,128)(2,1)S(1)} %bitcast.12), custom_call_target="tpu_custom_call" | custom-call | flops 2359296 | bytes 18874368 | tf_op jit(solution)/shard_map/scale/pallas_call | solution.py:443
Async XLA Ops:
  0.6 2.2 %copy-start.1 = (bf16[1,512,4096]{2,1,0:T(8,128)(2,1)S(1)}, bf16[1,512,4096]{2,1,0:T(8,128)(2,1)}, u32[]{:S(2)}) copy-start(bf16[1,512,4096]{2,1,0:T(8,128)(2,1)} %param.10) | copy-start | bytes 12582916
  2.8 1.4 copy-start.2
  4.2 1.1 copy-start.3
  5.3 0.7 copy-start.4
  6.0 1.4 copy-start.5
  7.4 141.6 %copy-start = (bf16[1,384,6144]{2,1,0:T(8,128)(2,1)S(1)}, bf16[1,384,6144]{2,1,0:T(8,128)(2,1)}, u32[]{:S(2)}) copy-start(bf16[1,384,6144]{2,1,0:T(8,128)(2,1)} %param.9) | copy-start | bytes 14155780
